TPU v7x, 8 devices: a whole 2x2x1 slice. The times are simulated.
8 devices in a mesh: dp: 1 (over z), sh: 8 (over y, x, core).
Axes of the slice: x: 2, y: 2, z: 1, core: 2. Of those that a mesh axis runs over, the one named last changes fastest.
Arguments:
- k_prefill: bfloat16 [16, 5120, 16, 128], P('dp', None, 'sh')
- v_prefill: bfloat16 [16, 5120, 16, 128], P('dp', None, 'sh')
- lengths: int32 [16], P('dp')
- residual: bfloat16 [16, 4608], P(('dp', 'sh'))
- norm_gain: bfloat16 [4608], replicated
- w_query: bfloat16 [4608, 4096], replicated
- w_key: bfloat16 [4608, 2048], replicated
- w_value: bfloat16 [4608, 2048], replicated
- w_out: bfloat16 [4096, 4608], replicated
Outputs:
- output 1: bfloat16 [16, 4608], P(('dp', 'sh'))
- output 2: bfloat16 [16, 4096, 16, 128], P(('dp', 'sh'))
- output 3: bfloat16 [16, 4096, 16, 128], P(('dp', 'sh'))
All inputs are finite; a program needn't handle non-finite values.
Results may differ from a plain program's by a relative error of at most 0.00409.
Values are sent between devices in bfloat16 or wider.
A program may use at most 1 GiB of HBM per device.

v0:
```python
import jax
import jax.numpy as jnp
from jax import lax
from jax.sharding import PartitionSpec as P

WINDOW = 4096
THETA = 10000.0
EPS = 1e-5


def rolling_rows(prefill, lengths):
    def one_row(row_vals, row_len):
        first_pos = jnp.maximum(row_len - WINDOW, 0)
        win_vals = lax.dynamic_slice_in_dim(row_vals, first_pos, WINDOW, axis=0)
        positions = first_pos + jnp.arange(WINDOW, dtype=jnp.int32)
        win_vals = jnp.where((positions < row_len)[:, None, None], win_vals, jnp.zeros((), win_vals.dtype))
        doubled = jnp.concatenate([win_vals, win_vals], axis=0)
        return lax.dynamic_slice_in_dim(doubled, WINDOW - first_pos % WINDOW, WINDOW, axis=0)
    return jax.vmap(one_row)(prefill, lengths)


def rotate(heads, positions):
    head_dim = heads.shape[-1]
    half_dim = head_dim // 2
    inv_freq = THETA ** (-2.0 * jnp.arange(half_dim, dtype=jnp.float32) / head_dim)
    angles = positions.astype(jnp.float32).reshape(positions.shape + (1,) * (heads.ndim - 1)) * inv_freq
    cos_part = jnp.cos(angles)
    sin_part = jnp.sin(angles)
    first_half = heads[..., :half_dim].astype(jnp.float32)
    second_half = heads[..., half_dim:].astype(jnp.float32)
    return jnp.concatenate([first_half * cos_part - second_half * sin_part, second_half * cos_part + first_half * sin_part], axis=-1).astype(jnp.bfloat16)


def decode_rows(residual, lengths, k_cache, v_cache, norm_gain, w_query, w_key, w_value, w_out):
    num_rows = residual.shape[0]
    kv_heads = k_cache.shape[2]
    head_dim = k_cache.shape[3]
    q_group = w_query.shape[1] // (kv_heads * head_dim)
    resid_f32 = residual.astype(jnp.float32)
    inv_rms = lax.rsqrt(jnp.mean(resid_f32 * resid_f32, axis=-1, keepdims=True) + EPS)
    normed = (resid_f32 * inv_rms * norm_gain.astype(jnp.float32)).astype(jnp.bfloat16)
    q_heads = jnp.dot(normed, w_query, preferred_element_type=jnp.float32).astype(jnp.bfloat16).reshape(num_rows, kv_heads, q_group, head_dim)
    k_new = jnp.dot(normed, w_key, preferred_element_type=jnp.float32).astype(jnp.bfloat16).reshape(num_rows, kv_heads, head_dim)
    v_new = jnp.dot(normed, w_value, preferred_element_type=jnp.float32).astype(jnp.bfloat16).reshape(num_rows, kv_heads, head_dim)
    q_heads = rotate(q_heads, lengths)
    k_new = rotate(k_new, lengths)
    slot_ids = jnp.arange(WINDOW, dtype=jnp.int32)
    new_slot = (slot_ids[None, :] == (lengths % WINDOW)[:, None])[:, :, None, None]
    k_cache = jnp.where(new_slot, k_new[:, None], k_cache)
    v_cache = jnp.where(new_slot, v_new[:, None], v_cache)
    live_slot = (lengths[:, None] - jnp.remainder(lengths[:, None] - slot_ids[None, :], WINDOW)) >= 0
    scores = jnp.einsum('rkgd,rwkd->rkgw', q_heads, k_cache, preferred_element_type=jnp.float32) / head_dim ** 0.5
    scores = jnp.where(live_slot[:, None, None, :], scores, -jnp.inf)
    exp_scores = jnp.exp(scores - jnp.max(scores, axis=-1, keepdims=True))
    weights = (exp_scores / jnp.sum(exp_scores, axis=-1, keepdims=True)).astype(jnp.bfloat16)
    attn_out = jnp.einsum('rkgw,rwkd->rkgd', weights, v_cache, preferred_element_type=jnp.float32).astype(jnp.bfloat16).reshape(num_rows, kv_heads * q_group * head_dim)
    resid_out = (resid_f32 + jnp.dot(attn_out, w_out, preferred_element_type=jnp.float32)).astype(jnp.bfloat16)
    return resid_out, k_cache, v_cache


def solution(mesh):
    head_spec = P('dp', None, 'sh', None)
    row_spec = P(('dp', 'sh'))
    full_spec = P(None, None)

    def per_device(k_prefill, v_prefill, lengths, residual, norm_gain, w_query, w_key, w_value, w_out):
        num_rows = residual.shape[0]
        my_lengths = lax.dynamic_slice_in_dim(lengths, lax.axis_index('sh') * num_rows, num_rows)
        k_rows = lax.all_to_all(k_prefill, 'sh', 0, 2, tiled=True)
        v_rows = lax.all_to_all(v_prefill, 'sh', 0, 2, tiled=True)
        k_cache = rolling_rows(k_rows, my_lengths)
        v_cache = rolling_rows(v_rows, my_lengths)
        return decode_rows(residual, my_lengths, k_cache, v_cache, norm_gain, w_query, w_key, w_value, w_out)
    return jax.shard_map(per_device, mesh=mesh, in_specs=(head_spec, head_spec, P('dp'), P(('dp', 'sh'), None), P(None), full_spec, full_spec, full_spec, full_spec), out_specs=(P(('dp', 'sh'), None), row_spec, row_spec), check_vma=False)
```

profile of v0, /device:TPU:0, one launch (start us, length us, event | category | flops | bytes accessed | tf_op | source)
XLA Modules:
  0.0 1335.4 jit_solution(9252022709586847889)
XLA Ops:
  0.6 466.0 %all_to_all.36 = bf16[16,5120,2,128]{3,2,1,0:T(2,128)(2,1)} all-to-all(bf16[16,5120,2,128]{3,2,1,0:T(2,128)(2,1)} %param.10), channel_id=1, replica_groups=mesh['dp'=1,'sh'=8] {'sh'}, dimensions={0} | all-to-all | bytes 83886080 | tf_op jit(solution)/shard_map/all_to_all | solution.py:70
  466.6 6.7 all-to-all-start
  474.4 7.7 fusion.17
  482.1 7.7 fusion.18
  490.5 14.3 %convolution_convert_fusion = bf16[2,4096]{1,0:T(2,128)(2,1)S(1)} fusion(bf16[4608,4096]{1,0:T(8,128)(2,1)} %param.14, bf16[2,4608]{1,0:T(2,128)(2,1)S(1)} %copy-done, f32[2]{0:T(128)S(1)} %add_rsqrt_fusion, f32[4608]{0:T(1024)S(1)} %convert_element_type.50), kind=kOutput, calls=%fused_computation.25 | convolution fusion | flops 75542528 | bytes 37801992 | tf_op jit(solution)/shard_map/dot_general | solution.py:42
  506.5 0.8 fusion.29
  507.3 33.5 %copy.36 = bf16[8,2,5120,2,128]{4,3,0,2,1:T(2,128)(2,1)} copy(bf16[8,2,5120,2,128]{4,3,2,1,0:T(2,128)(2,1)} %bitcast.53) | data formatting | bytes 83886080 | tf_op jit(solution)/shard_map/all_to_all | solution.py:70
  540.8 11.2 broadcast.224.clone.1
  552.0 32.7 %while.6 = (s32[]{:T(128)}, bf16[2,5120,16,128]{3,2,1,0:T(8,128)(2,1)}, s32[2,4]{1,0:T(2,128)S(1)}, bf16[2,4096,16,128]{3,2,1,0:T(8,128)(2,1)}, s32[]{:T(128)}) while((s32[]{:T(128)}, bf16[2,5120,16,128]{3,2,1,0:T(8,128)(2,1)}, s32[2,4]{1,0:T(2,128)S(1)}, bf16[2,4096,16,128]{3,2,1,0:T(8,128)(2,1)}, s32[]{:T(128)}) %tuple.104), condition=%wide.while_cond.2, body=%wide.while_body.2.sunk | while | flops 2 | bytes 33556080 | solution.py:14
  552.6 15.8 %dynamic-slice_dynamic-update-slice_fusion.10 = bf16[2,4096,16,128]{3,2,1,0:T(8,128)(2,1)} fusion(bf16[2,4096,16,128]{3,2,1,0:T(8,128)(2,1)} %get-tuple-element.287, s32[]{:T(128)} %get-tuple-element.284, bf16[2,5120,16,128]{3,2,1,0:T(8,128)(2,1)} %get-tuple-element.290, s32[]{:T(128)} %bitcast.47, s32[]{:T(128)} %bitcast.48), kind=kLoop, calls=%fused_computation.4.clone.1 | loop fusion | bytes 33555968 | tf_op jit(solution)/shard_map/vmap()/gather
  568.9 15.8 %dynamic-slice_dynamic-update-slice_fusion.10 = bf16[2,4096,16,128]{3,2,1,0:T(8,128)(2,1)} fusion(bf16[2,4096,16,128]{3,2,1,0:T(8,128)(2,1)} %get-tuple-element.287, s32[]{:T(128)} %get-tuple-element.284, bf16[2,5120,16,128]{3,2,1,0:T(8,128)(2,1)} %get-tuple-element.290, s32[]{:T(128)} %bitcast.47, s32[]{:T(128)} %bitcast.48), kind=kLoop, calls=%fused_computation.4.clone.1 | loop fusion | bytes 33555968 | tf_op jit(solution)/shard_map/vmap()/gather
  584.7 342.5 %all-to-all-done = bf16[16,5120,2,128]{3,2,1,0:T(2,128)(2,1)} async-done(((bf16[16,5120,2,128]{3,2,1,0:T(2,128)(2,1)}), bf16[16,5120,2,128]{3,2,1,0:T(2,128)(2,1)}, u32[]{:S(2)}, u32[]{:S(2)}) %all-to-all-start) | async-done | bytes 41943072 | tf_op jit(solution)/shard_map/all_to_all | solution.py:69
  927.2 33.5 %copy.31 = bf16[8,2,5120,2,128]{4,3,0,2,1:T(2,128)(2,1)} copy(bf16[8,2,5120,2,128]{4,3,2,1,0:T(2,128)(2,1)} %bitcast) | data formatting | bytes 83886080 | tf_op jit(solution)/shard_map/all_to_all | solution.py:69
  960.7 11.2 broadcast.224.clone
  971.9 32.9 %while.4 = (s32[]{:T(128)}, bf16[2,5120,16,128]{3,2,1,0:T(8,128)(2,1)}, s32[2,4]{1,0:T(2,128)S(1)}, bf16[2,4096,16,128]{3,2,1,0:T(8,128)(2,1)}, s32[]{:T(128)}) while((s32[]{:T(128)}, bf16[2,5120,16,128]{3,2,1,0:T(8,128)(2,1)}, s32[2,4]{1,0:T(2,128)S(1)}, bf16[2,4096,16,128]{3,2,1,0:T(8,128)(2,1)}, s32[]{:T(128)}) %tuple.107), condition=%wide.while_cond, body=%wide.while_body.sunk | while | flops 2 | bytes 33556080 | solution.py:14
  972.5 15.8 %dynamic-slice_dynamic-update-slice_fusion.8 = bf16[2,4096,16,128]{3,2,1,0:T(8,128)(2,1)} fusion(bf16[2,4096,16,128]{3,2,1,0:T(8,128)(2,1)} %get-tuple-element.272, s32[]{:T(128)} %get-tuple-element.269, bf16[2,5120,16,128]{3,2,1,0:T(8,128)(2,1)} %get-tuple-element.275, s32[]{:T(128)} %bitcast.43, s32[]{:T(128)} %bitcast.44), kind=kLoop, calls=%fused_computation.clone.1 | loop fusion | bytes 33555968 | tf_op jit(solution)/shard_map/vmap()/gather
  989.0 15.8 %dynamic-slice_dynamic-update-slice_fusion.8 = bf16[2,4096,16,128]{3,2,1,0:T(8,128)(2,1)} fusion(bf16[2,4096,16,128]{3,2,1,0:T(8,128)(2,1)} %get-tuple-element.272, s32[]{:T(128)} %get-tuple-element.269, bf16[2,5120,16,128]{3,2,1,0:T(8,128)(2,1)} %get-tuple-element.275, s32[]{:T(128)} %bitcast.43, s32[]{:T(128)} %bitcast.44), kind=kLoop, calls=%fused_computation.clone.1 | loop fusion | bytes 33555968 | tf_op jit(solution)/shard_map/vmap()/gather
  1004.8 44.7 %broadcast_select_fusion.1 = (bf16[2,4096,16,128]{3,2,1,0:T(8,128)(2,1)}, bf16[2,4096,16,128]{3,2,1,0:T(8,128)(2,1)}) fusion(bf16[2,4096,16,128]{3,2,1,0:T(8,128)(2,1)} %get-tuple-element.10, pred[2,4096]{1,0:T(4,128)(4,1)S(1)} %copy-done.3, bf16[2,4096,16,128]{3,2,1,0:T(8,128)(2,1)} %get-tuple-element.26), kind=kLoop, calls=%fused_computation.16 | loop fusion | flops 33554432 | bytes 134225920 | tf_op jit(solution)/shard_map/vmap(jit(_where))/select_n | solution.py:16
  1049.5 44.6 %pad_maximum_fusion.1 = bf16[2,8192,16,128]{3,2,1,0:T(8,128)(2,1)} fusion(bf16[2,4096,16,128]{3,2,1,0:T(8,128)(2,1)} %get-tuple-element.132), kind=kLoop, calls=%fused_computation.10 | loop fusion | flops 33554432 | bytes 100663296 | tf_op jit(solution)/shard_map/vmap()/concatenate | solution.py:17
  1094.1 11.2 broadcast.224.clone.3
  1105.3 33.0 %while.7 = (s32[]{:T(128)}, bf16[2,8192,16,128]{3,2,1,0:T(8,128)(2,1)}, s32[2,4]{1,0:T(2,128)S(1)}, bf16[2,4096,16,128]{3,2,1,0:T(8,128)(2,1)}, s32[]{:T(128)}) while((s32[]{:T(128)}, bf16[2,8192,16,128]{3,2,1,0:T(8,128)(2,1)}, s32[2,4]{1,0:T(2,128)S(1)}, bf16[2,4096,16,128]{3,2,1,0:T(8,128)(2,1)}, s32[]{:T(128)}) %tuple.105), condition=%wide.while_cond.3, body=%wide.while_body.3.sunk | while | flops 2 | bytes 33556080 | solution.py:18
  1106.0 15.8 %dynamic-slice_dynamic-update-slice_fusion.11 = bf16[2,4096,16,128]{3,2,1,0:T(8,128)(2,1)} fusion(bf16[2,4096,16,128]{3,2,1,0:T(8,128)(2,1)} %get-tuple-element.317, s32[]{:T(128)} %get-tuple-element.314, bf16[2,8192,16,128]{3,2,1,0:T(8,128)(2,1)} %get-tuple-element.320, s32[]{:T(128)} %bitcast.49, s32[]{:T(128)} %bitcast.50), kind=kLoop, calls=%fused_computation.6.clone.1 | loop fusion | bytes 33555968 | tf_op jit(solution)/shard_map/vmap()/gather
  1122.4 15.8 %dynamic-slice_dynamic-update-slice_fusion.11 = bf16[2,4096,16,128]{3,2,1,0:T(8,128)(2,1)} fusion(bf16[2,4096,16,128]{3,2,1,0:T(8,128)(2,1)} %get-tuple-element.317, s32[]{:T(128)} %get-tuple-element.314, bf16[2,8192,16,128]{3,2,1,0:T(8,128)(2,1)} %get-tuple-element.320, s32[]{:T(128)} %bitcast.49, s32[]{:T(128)} %bitcast.50), kind=kLoop, calls=%fused_computation.6.clone.1 | loop fusion | bytes 33555968 | tf_op jit(solution)/shard_map/vmap()/gather
  1138.2 44.6 %pad_maximum_fusion = bf16[2,8192,16,128]{3,2,1,0:T(8,128)(2,1)} fusion(bf16[2,4096,16,128]{3,2,1,0:T(8,128)(2,1)} %get-tuple-element.131), kind=kLoop, calls=%fused_computation.9 | loop fusion | flops 33554432 | bytes 100663296 | tf_op jit(solution)/shard_map/vmap()/concatenate | solution.py:17
  1182.9 11.4 broadcast.224.clone.2
  1194.2 33.0 %while.5 = (s32[]{:T(128)}, bf16[2,8192,16,128]{3,2,1,0:T(8,128)(2,1)}, s32[2,4]{1,0:T(2,128)S(1)}, bf16[2,4096,16,128]{3,2,1,0:T(8,128)(2,1)}, s32[]{:T(128)}) while((s32[]{:T(128)}, bf16[2,8192,16,128]{3,2,1,0:T(8,128)(2,1)}, s32[2,4]{1,0:T(2,128)S(1)}, bf16[2,4096,16,128]{3,2,1,0:T(8,128)(2,1)}, s32[]{:T(128)}) %tuple.106), condition=%wide.while_cond.1, body=%wide.while_body.1.sunk | while | flops 2 | bytes 33556080 | solution.py:18
  1194.9 15.8 %dynamic-slice_dynamic-update-slice_fusion.9 = bf16[2,4096,16,128]{3,2,1,0:T(8,128)(2,1)} fusion(bf16[2,4096,16,128]{3,2,1,0:T(8,128)(2,1)} %get-tuple-element.302, s32[]{:T(128)} %get-tuple-element.299, bf16[2,8192,16,128]{3,2,1,0:T(8,128)(2,1)} %get-tuple-element.305, s32[]{:T(128)} %bitcast.45, s32[]{:T(128)} %bitcast.46), kind=kLoop, calls=%fused_computation.2.clone.1 | loop fusion | bytes 33555968 | tf_op jit(solution)/shard_map/vmap()/gather
  1211.4 15.8 %dynamic-slice_dynamic-update-slice_fusion.9 = bf16[2,4096,16,128]{3,2,1,0:T(8,128)(2,1)} fusion(bf16[2,4096,16,128]{3,2,1,0:T(8,128)(2,1)} %get-tuple-element.302, s32[]{:T(128)} %get-tuple-element.299, bf16[2,8192,16,128]{3,2,1,0:T(8,128)(2,1)} %get-tuple-element.305, s32[]{:T(128)} %bitcast.45, s32[]{:T(128)} %bitcast.46), kind=kLoop, calls=%fused_computation.2.clone.1 | loop fusion | bytes 33555968 | tf_op jit(solution)/shard_map/vmap()/gather
  1227.3 44.7 %broadcast_select_fusion.3 = (bf16[2,4096,16,128]{3,2,1,0:T(8,128)(2,1)}, bf16[2,4096,16,128]{3,2,1,0:T(8,128)(2,1)}) fusion(bf16[2,4096,16,128]{3,2,1,0:T(8,128)(2,1)} %get-tuple-element.18, pred[2,4096]{1,0:T(4,128)(4,1)S(1)} %copy-done.2, bf16[2,16,128]{2,1,0:T(8,128)(2,1)S(1)} %copy-done.4, bf16[2,4096,16,128]{3,2,1,0:T(8,128)(2,1)} %get-tuple-element.34, ...), kind=kLoop, calls=%fused_computation.18 | loop fusion | flops 33554432 | bytes 134242304 | tf_op jit(solution)/shard_map/jit(_where)/select_n | solution.py:49
  1272.0 19.7 %fusion.47 = (f32[2,16,2]{2,1,0:T(8,128)S(1)}, f32[2,16,2,4096]{3,2,1,0:T(2,128)S(1)}) fusion(bf16[2,4096,16,128]{3,2,1,0:T(8,128)(2,1)} %get-tuple-element.129, pred[2,4096]{1,0:T(4,128)(4,1)S(1)} %copy-done.7, bf16[2,16,2,128]{3,1,2,0:T(8,128)(2,1)S(1)} %copy-done.6), kind=kOutput, calls=%fused_computation.88 | convolution fusion | flops 68161536 | bytes 34627840 | tf_op jit(solution)/shard_map/sub | solution.py:54
  1291.6 28.8 %fusion.14 = bf16[2,16,2,128]{3,2,1,0:T(2,128)(2,1)S(1)} fusion(bf16[2,4096,16,128]{3,2,1,0:T(8,128)(2,1)} %get-tuple-element.130, f32[2,16,2,4096]{3,2,1,0:T(2,128)S(1)} %get-tuple-element.146, f32[2,16,2]{2,1,0:T(8,128)S(1)} %get-tuple-element.145), kind=kOutput, calls=%fused_computation.28 | convolution fusion | flops 67641344 | bytes 34619648 | tf_op jit(solution)/shard_map/rkgw,rwkd->rkgd/dot_general | solution.py:56
  1320.5 14.9 %fusion.5 = bf16[2,4608]{1,0:T(2,128)(2,1)} fusion(bf16[2,4096]{1,0:T(2,128)(2,1)S(1)} %reshape.259, bf16[4096,4608]{1,0:T(8,128)(2,1)} %param.17, bf16[2,4608]{1,0:T(2,128)(2,1)S(1)} %copy-done.1), kind=kOutput, calls=%fused_computation.20 | convolution fusion | flops 75525120 | bytes 37801984 | tf_op jit(solution)/shard_map/dot_general | solution.py:57
  (58 shorter events, 8.6 us)
Async XLA Ops:
  466.6 6.7 copy-start.10
  466.6 7.6 copy-start.8
  466.6 7.6 copy-start
  466.6 460.6 %all-to-all-start = ((bf16[16,5120,2,128]{3,2,1,0:T(2,128)(2,1)}), bf16[16,5120,2,128]{3,2,1,0:T(2,128)(2,1)}, u32[]{:S(2)}, u32[]{:S(2)}) async-start(bf16[16,5120,2,128]{3,2,1,0:T(2,128)(2,1)} %param.9), calls=%async_computation | async-start | bytes 83886080 | tf_op jit(solution)/shard_map/all_to_all | solution.py:69
  971.9 32.9 %copy-start.3 = (pred[2,4096]{1,0:T(4,128)(4,1)S(1)}, pred[2,4096]{1,0:T(4,128)(4,1)}, u32[]{:S(2)}) copy-start(pred[2,4096]{1,0:T(4,128)(4,1)} %get-tuple-element.138) | copy-start | bytes 24580
  1094.1 11.2 copy-start.9
  1194.2 33.0 %copy-start.2 = (pred[2,4096]{1,0:T(4,128)(4,1)S(1)}, pred[2,4096]{1,0:T(4,128)(4,1)}, u32[]{:S(2)}) copy-start(pred[2,4096]{1,0:T(4,128)(4,1)} %get-tuple-element.147) | copy-start | bytes 24580
  1194.2 33.0 %copy-start.4 = (bf16[2,16,128]{2,1,0:T(8,128)(2,1)S(1)}, bf16[2,16,128]{2,1,0:T(8,128)(2,1)}, u32[]{:S(2)}) copy-start(bf16[2,16,128]{2,1,0:T(8,128)(2,1)} %pad_maximum_fusion.3) | copy-start | bytes 24580
  1194.2 33.0 %copy-start.5 = (bf16[1,2,16,128]{3,2,1,0:T(8,128)(2,1)S(1)}, bf16[1,2,16,128]{3,2,1,0:T(8,128)(2,1)}, u32[]{:S(2)}) copy-start(bf16[1,2,16,128]{3,2,1,0:T(8,128)(2,1)} %copy.66) | copy-start | bytes 24580
  1227.2 44.7 %copy-start.6 = (bf16[2,16,2,128]{3,1,2,0:T(8,128)(2,1)S(1)}, bf16[2,16,2,128]{3,1,2,0:T(8,128)(2,1)}, u32[]{:S(2)}) copy-start(bf16[2,16,2,128]{3,1,2,0:T(8,128)(2,1)} %pad_maximum_fusion.2) | copy-start | bytes 49156
  1227.2 44.7 %copy-start.7 = (pred[2,4096]{1,0:T(4,128)(4,1)S(1)}, pred[2,4096]{1,0:T(4,128)(4,1)}, u32[]{:S(2)}) copy-start(pred[2,4096]{1,0:T(4,128)(4,1)} %get-tuple-element.137) | copy-start | bytes 24580
  1272.0 48.5 %copy-start.1 = (bf16[2,4608]{1,0:T(2,128)(2,1)S(1)}, bf16[2,4608]{1,0:T(2,128)(2,1)}, u32[]{:S(2)}) copy-start(bf16[2,4608]{1,0:T(2,128)(2,1)} %param.12) | copy-start | bytes 55300
where the time goes:
time: 1340 us
  blocking collectives  466 us (35%)
  waiting for transfers between devices  342 us (26%)
  local copies, waits for them, and re-layouts  245 us (18%)
  other arithmetic  181 us (14%)
  matrix products  93.2 us (7%)
    all_to_all x1, blocking collectives, per_device(): v_rows = lax.all_to_all(v_prefill, 'sh', 0, 2, tiled=True)  466 us
    all_to_all x1, waiting for transfers between devices, per_device(): k_rows = lax.all_to_all(k_prefill, 'sh', 0, 2, tiled=True)  342 us
    gather x24, local copies, waits for them, and re-layouts  132 us
    concatenate x2, other arithmetic, one_row(): doubled = jnp.concatenate([win_vals, win_vals], axis=0)  89.2 us
    unnamed x31, local copies, waits for them, and re-layouts  46.3 us
    select_n x1, other arithmetic, decode_rows(): k_cache = jnp.where(new_slot, k_new[:, None], k_cache)  44.7 us
    select_n x1, other arithmetic, one_row(): jnp.where((positions < row_len)[:, None, None], win_vals, jnp.zeros((), w...  44.7 us
    all_to_all x1, local copies, waits for them, and re-layouts, per_device(): v_rows = lax.all_to_all(v_prefill, 'sh', 0, 2, tiled=True)  33.5 us
  transfers between devices with their start and end apart: 1, of which 1 were waited for; matrix products, arithmetic and copies ran while one was open for 8% of the time, Pallas kernels for 0%

commit v1 on v0

v1 whole, which is shorter than its diff:
```python
import functools

import jax
import jax.numpy as jnp
from jax import lax
from jax.experimental import pallas as pl
from jax.experimental.pallas import tpu as pltpu
from jax.sharding import PartitionSpec as P

WINDOW = 4096
SEQ = 5120
BATCH = 16
KVH = 16
HD = 128
THETA = 10000.0
EPS = 1e-5
MESH = pl.DeviceIdType.MESH

BLK = 128
NBLK = WINDOW // BLK
CHIP_ROWS = 4
GRAIN = 32
GRAINS = CHIP_ROWS * WINDOW // GRAIN
CSLOTS = 256
MAXCHUNKS = CHIP_ROWS * WINDOW // CSLOTS
LEVELS = (24, 30, 34) + tuple(range(37, 60)) + (61, MAXCHUNKS)
AHEAD = 8
ARRIVE = 32
LAGS = (0, 2, 3, 7)
WCOLS = 256
WBUF = 4
WPART = 8
KSTEP = 512


def row_grains(n):
    return (jnp.minimum(n, WINDOW) + (GRAIN - 1)) // GRAIN


def source_table(lengths):
    n = lengths.reshape(4, CHIP_ROWS)
    count = row_grains(n)
    grain = jnp.arange(GRAINS, dtype=jnp.int32)[None, :]
    begin = jnp.zeros((4, 1), jnp.int32)
    at = grain
    place = jnp.zeros((4, GRAINS), jnp.int32)
    length = n[:, 0:1]
    for r in range(1, CHIP_ROWS):
        begin = begin + count[:, r - 1:r]
        after = grain >= begin
        at = jnp.where(after, grain - begin, at)
        place = jnp.where(after, r * SEQ, place)
        length = jnp.where(after, n[:, r:r + 1], length)
    at = jnp.minimum(at * GRAIN, WINDOW - GRAIN)
    wrapped = jnp.clip(length - WINDOW - at, 0, GRAIN)
    return ((place + at) * 64 + wrapped).reshape(-1)


def exchange_kernel(steps, tab_ref, x_ref, g_ref, k_ref, v_ref, wq_ref, wk_ref, wv_ref,
                    r_ref, p_ref, rows0, rows1, rows2, rows3, stage, wbuf, normed,
                    load_sem, send_sem, recv_sem, own_sem, fsend_sem, frecv_sem, w_sem):
    me = lax.axis_index("sh")
    core = lax.rem(me, 2)
    my_chip = lax.div(me, 2)
    chip_x = lax.rem(my_chip, 2)
    chip_y = lax.div(my_chip, 2)
    partner = me + 1 - 2 * core
    chips = ((1 - chip_y) * 2 + (1 - chip_x), (1 - chip_y) * 2 + chip_x, chip_y * 2 + (1 - chip_x), my_chip)
    peers = [c * 2 + core for c in chips]
    rows = (rows0, rows1, rows2, rows3)
    total = 2 * steps

    def load(ref, j):
        flat = CHIP_ROWS * SEQ
        return pltpu.make_async_copy(ref.at[pl.ds(chips[j] * flat, flat)], rows[j], load_sem.at[j])

    load(k_ref, 0).start()
    barrier = pltpu.get_barrier_semaphore()
    for p in peers[:3] + [partner]:
        pl.semaphore_signal(barrier, inc=1, device_id={"sh": p}, device_id_type=MESH)
    pl.semaphore_wait(barrier, 4)

    def place(c):
        phase = (c >= steps).astype(jnp.int32)
        return phase, pl.ds((c - phase * steps) * CSLOTS, CSLOTS), lax.rem(c, AHEAD)

    def send(c, j):
        phase, slots, slot = place(c)
        return pltpu.make_async_remote_copy(
            stage.at[j, slot], r_ref.at[phase, slots, me], send_sem.at[j, slot], recv_sem.at[j, lax.rem(c, ARRIVE)],
            device_id={"sh": peers[j]}, device_id_type=MESH)

    def own(c):
        phase, slots, slot = place(c)
        return pltpu.make_async_copy(stage.at[3, slot], r_ref.at[phase, slots, me], own_sem.at[slot])

    def forward(c, j):
        phase, slots, _ = place(c)
        view = r_ref.at[phase, slots, peers[j]]
        return pltpu.make_async_remote_copy(
            view, view, fsend_sem, frecv_sem, device_id={"sh": partner}, device_id_type=MESH)

    def pack(c, j):
        first = chips[j] * GRAINS + jnp.where(c >= steps, c - steps, c) * (CSLOTS // GRAIN)
        slot = lax.rem(c, AHEAD)

        def piece(i, _):
            entry = tab_ref[first + i]
            at = lax.div(entry, 64)
            plain = rows[j][pl.ds(at, GRAIN)]
            wrapped = rows[j][pl.ds(jnp.minimum(at + WINDOW, CHIP_ROWS * SEQ - GRAIN), GRAIN)]
            pos = lax.broadcasted_iota(jnp.int32, (GRAIN, 2, HD), 0)
            stage[j, slot, pl.ds(i * GRAIN, GRAIN)] = jnp.where(pos < lax.rem(entry, 64), wrapped, plain)
            return 0
        lax.fori_loop(0, CSLOTS // GRAIN, piece, 0)

    def normalize():
        x = x_ref[...].astype(jnp.float32)
        inv_rms = lax.rsqrt(jnp.mean(x * x, axis=-1, keepdims=True) + EPS)
        normed[...] = (x * inv_rms * g_ref[...].astype(jnp.float32).reshape(1, -1)).astype(jnp.bfloat16)

    def project(first):
        def step(k, _):
            i = first + k
            for ref, lo, hi in ((wq_ref, 0, 16), (wk_ref, 16, 24), (wv_ref, 24, 32)):
                @pl.when(jnp.logical_and(k < WPART, jnp.logical_and(i >= lo, i < hi)))
                def _():
                    cols = pl.ds(pl.multiple_of((i - lo) * WCOLS, WCOLS), WCOLS)
                    pltpu.make_async_copy(ref.at[:, cols], wbuf.at[lax.rem(i, WBUF)], w_sem.at[lax.rem(i, WBUF)]).start()
            e = i - (WBUF - 1)

            @pl.when(k >= WBUF - 1)
            def _():
                slot = lax.rem(e, WBUF)
                pltpu.make_async_copy(wq_ref.at[:, pl.ds(0, WCOLS)], wbuf.at[slot], w_sem.at[slot]).wait()

                def part(kk, y):
                    at = pl.ds(pl.multiple_of(kk * KSTEP, KSTEP), KSTEP)
                    return y + jnp.dot(normed[:, at], wbuf[slot, at], preferred_element_type=jnp.float32)
                y = lax.fori_loop(0, 4608 // KSTEP, part, jnp.zeros((2, WCOLS), jnp.float32))
                p_ref[:, pl.ds(pl.multiple_of(e * WCOLS, WCOLS), WCOLS)] = y.astype(jnp.bfloat16)
            return 0
        lax.fori_loop(0, WPART + WBUF - 1, step, 0)

    def body(t, _):
        for j in range(4):
            c = t - LAGS[j]
            u = c - AHEAD

            @pl.when(jnp.logical_and(u >= 0, u < total))
            def _():
                if j < 3:
                    send(u, j).wait_send()
                else:
                    own(u).wait()
                    forward(u, 3).start()

            @pl.when(jnp.logical_and(c >= 0, c < total))
            def _():
                @pl.when(jnp.logical_or(c == 0, c == steps))
                def _():
                    load(k_ref, j).wait()

                if j < 2:
                    @pl.when(c == 0)
                    def _():
                        for i in ((1, 2) if j == 0 else (3,)):
                            load(k_ref, i).start()
                pack(c, j)

                @pl.when(c == steps - 1)
                def _():
                    load(v_ref, j).start()
                if j < 3:
                    send(c, j).start()
                else:
                    own(c).start()

        @pl.when(t == 6)
        def _():
            normalize()

        @pl.when(jnp.logical_and(lax.rem(t, 8) == 7, t < 32))
        def _():
            project(t - 7)

        for j in range(3):
            u = t - LAGS[j] - AHEAD

            @pl.when(jnp.logical_and(u >= 0, u < total))
            def _():
                send(u, j).wait_recv()
                forward(u, j).start()
        return 0
    lax.fori_loop(0, total + AHEAD + LAGS[3], body, 0)

    view = r_ref.at[:, pl.ds(0, steps * CSLOTS), pl.ds(0, 4)]
    everything = pltpu.make_async_remote_copy(
        view, view, fsend_sem, frecv_sem, device_id={"sh": partner}, device_id_type=MESH)
    everything.wait()


def exchange(level, table, x, g, k, v, wq, wk, wv):
    hbm = pl.BlockSpec(memory_space=pl.ANY)
    vmem = pl.BlockSpec(memory_space=pltpu.VMEM)
    smem = pl.BlockSpec(memory_space=pltpu.SMEM)
    rows = pltpu.VMEM((CHIP_ROWS * SEQ, 2, HD), jnp.bfloat16)

    def branch(i, *args):
        return pl.pallas_call(
            functools.partial(exchange_kernel, LEVELS[i]),
            out_shape=(jax.ShapeDtypeStruct((2, CHIP_ROWS * WINDOW + BLK, 8, 2, HD), jnp.bfloat16),
                       jax.ShapeDtypeStruct((2, 8192), jnp.bfloat16)),
            in_specs=[smem, vmem, vmem] + [hbm] * 5,
            out_specs=(hbm, vmem),
            scratch_shapes=[
                rows, rows, rows, rows,
                pltpu.VMEM((4, AHEAD, CSLOTS, 2, HD), jnp.bfloat16),
                pltpu.VMEM((WBUF, 4608, WCOLS), jnp.bfloat16),
                pltpu.VMEM((2, 4608), jnp.bfloat16),
                pltpu.SemaphoreType.DMA((4,)),
                pltpu.SemaphoreType.DMA((3, AHEAD)), pltpu.SemaphoreType.DMA((3, ARRIVE)),
                pltpu.SemaphoreType.DMA((AHEAD,)),
                pltpu.SemaphoreType.DMA, pltpu.SemaphoreType.DMA,
                pltpu.SemaphoreType.DMA((WBUF,)),
            ],
            compiler_params=pltpu.CompilerParams(
                collective_id=i, has_side_effects=True, vmem_limit_bytes=62 * 2**20),
            name=f"exchange_{LEVELS[i]}",
        )(*args)
    return lax.switch(level, [functools.partial(branch, i) for i in range(len(LEVELS))],
                      table, x, g, k.reshape(BATCH * SEQ, 2, HD), v.reshape(BATCH * SEQ, 2, HD), wq, wk, wv)


NBUF = 8
LOOK = 5
COLS = BLK * KVH


def attend_kernel(len_ref, q_ref, kn_ref, vn_ref, r_ref, o_ref, kc_ref, vc_ref,
                  buf, zbuf, sc, mx, acc, in_sem, out_sem, zero_sem):
    me = lax.axis_index("sh")
    row0 = 2 * me
    base = CHIP_ROWS * (me // 2)
    lens = [len_ref[row0], len_ref[row0 + 1]]
    before = row_grains(len_ref[base]) + row_grains(len_ref[base + 1])
    start0 = jnp.where(me % 2 == 1, before, 0)
    starts = [start0, start0 + row_grains(lens[0])]
    acts = [jnp.where(n >= WINDOW, NBLK, n // BLK + 1) for n in lens]
    units = acts[0] + acts[1]

    def where_is(u):
        second = u >= acts[0]
        r = second.astype(jnp.int32)
        sig = jnp.where(second, u - acts[0], u)
        at = jnp.where(second, starts[1], starts[0]) * GRAIN + sig * BLK
        return r, sig, at, jnp.where(second, lens[1], lens[0])

    def in_copy(half, w, u):
        _, _, at, _ = where_is(u)
        return pltpu.make_async_copy(r_ref.at[half, pl.ds(at, BLK)], buf.at[w % NBUF], in_sem.at[w % NBUF])

    def out_copy(ref, w, u):
        r, sig, _, _ = where_is(u)
        return pltpu.make_async_copy(buf.at[w % NBUF], ref.at[r, pl.ds(sig * BLK, BLK)], out_sem.at[w % NBUF])

    def start_in(w):
        @pl.when(w < units)
        def _():
            in_copy(0, w, w).start()

        @pl.when(jnp.logical_and(w >= units, w < 2 * units))
        def _():
            in_copy(1, w, w - units).start()

    def wait_out(w):
        @pl.when(w >= 0)
        def _():
            out_copy(kc_ref, w, 0).wait()

    for w in range(LOOK):
        start_in(jnp.int32(w))

    zbuf[...] = jnp.zeros_like(zbuf)

    def zero_copies(r, sig):
        return [pltpu.make_async_copy(zbuf, ref.at[r, pl.ds(sig * BLK, BLK)], zero_sem.at[x])
                for x, ref in enumerate((kc_ref, vc_ref))]
    for r in range(2):
        def put_zero(sig, _, r=r):
            for c in zero_copies(r, sig):
                c.start()
            return 0
        lax.fori_loop(acts[r], NBLK, put_zero, 0)

    mx[...] = jnp.full_like(mx, -jnp.inf)
    acc[...] = jnp.zeros_like(acc)
    col = lax.broadcasted_iota(jnp.int32, (32, COLS), 1)
    rowid = lax.broadcasted_iota(jnp.int32, (32, COLS), 0)
    match = (rowid % KVH) == (col % KVH)
    col2 = lax.broadcasted_iota(jnp.int32, (2, COLS), 1) // KVH
    scale = 1.0 / HD ** 0.5

    def fix(slot, r, sig, n, new_ref):
        new_slot = n % WINDOW

        @pl.when(sig == new_slot // BLK)
        def _():
            here = sig * BLK + lax.broadcasted_iota(jnp.int32, (BLK, KVH, HD), 0)
            val = buf[slot]
            val = jnp.where(here > n, jnp.zeros_like(val), val)
            new = jnp.broadcast_to(new_ref[r][None], val.shape)
            buf[slot] = jnp.where(here == new_slot, new, val)

    def k_step(u, _):
        r, sig, _, n = where_is(u)
        slot = u % NBUF
        wait_out(u + LOOK - NBUF)
        start_in(u + LOOK)
        in_copy(0, u, u).wait()
        fix(slot, r, sig, n, kn_ref)
        kb = buf[slot].reshape(COLS, HD)
        s = lax.dot_general(q_ref[r], kb, (((1,), (1,)), ((), ())), preferred_element_type=jnp.float32)
        out_copy(kc_ref, u, u).start()
        s = jnp.where(match, s, 0.0)
        s = jnp.concatenate([jnp.sum(s[:KVH], axis=0, keepdims=True),
                             jnp.sum(s[KVH:], axis=0, keepdims=True)], axis=0)
        s = jnp.where(sig * BLK + col2 > n, -jnp.inf, s * scale)
        sc[u] = s
        mx[r] = jnp.maximum(mx[r], s)
        return 0
    lax.fori_loop(0, units, k_step, 0)

    def fold(x, op):
        y = x[:, :HD]
        for i in range(1, COLS // HD):
            y = op(y, x[:, i * HD:(i + 1) * HD])
        for sh in (16, 32, 64):
            y = op(y, pltpu.roll(y, sh, 1))
        return jnp.concatenate([y] * (COLS // HD), axis=1)

    for r in range(2):
        top = fold(mx[r], jnp.maximum)
        lo = 0 if r == 0 else acts[0]

        def exp_step(i, tot, top=top, lo=lo):
            e = jnp.exp(sc[lo + i] - top)
            sc[lo + i] = e
            return tot + e
        tot = lax.fori_loop(0, acts[r], exp_step, jnp.zeros((2, COLS), jnp.float32))
        mx[r] = fold(tot, jnp.add)

    def v_step(u, _):
        r, sig, _, n = where_is(u)
        w = u + units
        slot = w % NBUF
        wait_out(w + LOOK - NBUF)
        start_in(w + LOOK)
        in_copy(1, w, u).wait()
        fix(slot, r, sig, n, vn_ref)
        p = sc[u] / mx[r]
        wide = jnp.concatenate([jnp.broadcast_to(p[0:1], (KVH, COLS)),
                                jnp.broadcast_to(p[1:2], (KVH, COLS))], axis=0)
        wide = jnp.where(match, wide, 0.0).astype(jnp.bfloat16)
        vb = buf[slot].reshape(COLS, HD)
        acc[r] += jnp.dot(wide, vb, preferred_element_type=jnp.float32)
        out_copy(vc_ref, w, u).start()
        return 0
    lax.fori_loop(0, units, v_step, 0)
    o_ref[...] = acc[...].astype(o_ref.dtype)

    def drain(w, _):
        wait_out(w)
        return 0
    lax.fori_loop(2 * units + LOOK - NBUF, 2 * units, drain, 0)
    for r in range(2):
        def wait_zero(sig, _, r=r):
            for c in zero_copies(r, sig):
                c.wait()
            return 0
        lax.fori_loop(acts[r], NBLK, wait_zero, 0)


def attend(lengths, q, kn, vn, r):
    hbm = pl.BlockSpec(memory_space=pl.ANY)
    vmem = pl.BlockSpec(memory_space=pltpu.VMEM)
    cache = jax.ShapeDtypeStruct((2, WINDOW, KVH, HD), jnp.bfloat16)
    return pl.pallas_call(
        attend_kernel,
        out_shape=(jax.ShapeDtypeStruct((2, 32, HD), jnp.bfloat16), cache, cache),
        in_specs=[pl.BlockSpec(memory_space=pltpu.SMEM), vmem, vmem, vmem, hbm],
        out_specs=(vmem, hbm, hbm),
        scratch_shapes=[
            pltpu.VMEM((NBUF, BLK, KVH, HD), jnp.bfloat16),
            pltpu.VMEM((BLK, KVH, HD), jnp.bfloat16),
            pltpu.VMEM((2 * NBLK, 2, COLS), jnp.float32),
            pltpu.VMEM((2, 2, COLS), jnp.float32),
            pltpu.VMEM((2, 32, HD), jnp.float32),
            pltpu.SemaphoreType.DMA((NBUF,)), pltpu.SemaphoreType.DMA((NBUF,)),
            pltpu.SemaphoreType.DMA((2,)),
        ],
        name="attend",
    )(lengths, q, kn, vn, r.reshape(2, CHIP_ROWS * WINDOW + BLK, KVH, HD))


def rotate(heads, positions):
    half = HD // 2
    inv_freq = THETA ** (-2.0 * jnp.arange(half, dtype=jnp.float32) / HD)
    angles = positions.astype(jnp.float32).reshape(positions.shape + (1,) * (heads.ndim - 1)) * inv_freq
    cos_part = jnp.cos(angles)
    sin_part = jnp.sin(angles)
    first = heads[..., :half].astype(jnp.float32)
    second = heads[..., half:].astype(jnp.float32)
    return jnp.concatenate([first * cos_part - second * sin_part, second * cos_part + first * sin_part], axis=-1).astype(jnp.bfloat16)


def solution(mesh):
    head_spec = P('dp', None, 'sh', None)
    row_spec = P(('dp', 'sh'))
    full_spec = P(None, None)

    def per_device(k_prefill, v_prefill, lengths, residual, norm_gain, w_query, w_key, w_value, w_out):
        rows = residual.shape[0]
        mine = lax.dynamic_slice_in_dim(lengths, lax.axis_index('sh') * rows, rows)
        longest = jnp.max(jnp.sum(row_grains(lengths).reshape(4, CHIP_ROWS), axis=1)) * GRAIN
        level = jnp.sum(longest > jnp.asarray(LEVELS, jnp.int32) * CSLOTS).astype(jnp.int32)
        r, p = exchange(level, source_table(lengths), residual, norm_gain, k_prefill, v_prefill, w_query, w_key, w_value)
        q = p[:, :4096].reshape(rows, KVH, 2, HD)
        kn = p[:, 4096:6144].reshape(rows, KVH, HD)
        vn = p[:, 6144:].reshape(rows, KVH, HD)
        q = rotate(q, mine).transpose(0, 2, 1, 3).reshape(rows, 2 * KVH, HD)
        kn = rotate(kn, mine)
        o, kc, vc = attend(lengths, q, kn, vn, r)
        o = o.reshape(rows, 2, KVH, HD).transpose(0, 2, 1, 3).reshape(rows, 2 * KVH * HD)
        out = (residual.astype(jnp.float32) + jnp.dot(o, w_out, preferred_element_type=jnp.float32)).astype(jnp.bfloat16)
        return out, kc, vc
    return jax.shard_map(per_device, mesh=mesh, in_specs=(head_spec, head_spec, P('dp'), P(('dp', 'sh'), None), P(None), full_spec, full_spec, full_spec, full_spec), out_specs=(P(('dp', 'sh'), None), row_spec, row_spec), check_vma=False)
```

time: 1340 us -> 752 us (0.56)
  Pallas kernels: 0 us -> 735 us
  blocking collectives: 466 us -> 0 us
  waiting for transfers between devices: 342 us -> 0 us
  local copies, waits for them, and re-layouts: 245 us -> 2.75 us
  other arithmetic: 181 us -> 5.25 us
  matrix products: 93.2 us -> 14.9 us
    pallas_call x0 -> x2, Pallas kernels: none -> 735 us  [the longest x1 699 us: branch(): pl.pallas_call(functools.partial(exchange_kernel, LEVELS[i]), out_shape=(...]
    all_to_all x1 -> x0, blocking collectives: 466 us -> none  [per_device(): v_rows = lax.all_to_all(v_prefill, 'sh', 0, 2, tiled=True)]
    all_to_all x1 -> x0, waiting for transfers between devices: 342 us -> none  [per_device(): k_rows = lax.all_to_all(k_prefill, 'sh', 0, 2, tiled=True)]
    gather x24 -> x0, local copies, waits for them, and re-layouts: 132 us -> none
    concatenate x4 -> x2, other arithmetic: 90.6 us -> 1.37 us  [rotate(): jnp.concatenate([first * cos_part - second * sin_part, second * cos_part...]
    select_n x3 -> x2, other arithmetic: 89.4 us -> 0.68 us  [row_grains(): return (jnp.minimum(n, WINDOW) + (GRAIN - 1)) // GRAIN]
    all_to_all x2 -> x0, local copies, waits for them, and re-layouts: 67 us -> none  [the longest x1 33.5 us: per_device(): v_rows = lax.all_to_all(v_prefill, 'sh', 0, 2, tiled=True)]
    dot_general x5 -> x1, matrix products: 73.6 us -> 14.9 us  [per_device(): jnp.dot(o, w_out, preferred_element_type=jnp.float32)]
  transfers between devices with their start and end apart: 1 -> 0, of which waited for: 1 -> 0; matrix products, arithmetic and copies ran while one was open for 8% -> 0% of each run, Pallas kernels for 0% -> 0%
where the time goes in v1:
time: 752 us; the launch traced here: 761 us
  Pallas kernels  735 us (98%)
  matrix products  14.9 us (2%)
    pallas_call x1, Pallas kernels, branch(): pl.pallas_call(functools.partial(exchange_kernel, LEVELS[i]), out_shape=(...  699 us
    pallas_call x1, Pallas kernels, attend(): pl.pallas_call(attend_kernel, out_shape=(jax.ShapeDtypeStruct((2, 32, HD)...  36.3 us

profile of v1, /device:TPU:0, one launch (start us, length us, event | category | flops | bytes accessed | tf_op | source)
XLA Modules:
  0.0 760.7 jit_solution(16462745545289299289)
XLA Ops:
  0.6 0.7 reshape.676
  1.4 0.2 add_reduce_fusion
  1.6 0.1 broadcast_bitcast_fusion.112
  1.7 0.1 broadcast_bitcast_fusion.114
  1.8 0.7 and_select_fusion
  2.5 0.1 reshape.675
  2.6 0.1 reduce_sum.18
  2.7 0.6 reduce_max.9
  4.0 1.3 fusion.15
  5.9 0.0 copy-start.1
  5.9 700.3 %conditional.1 = (bf16[2,8192]{1,0:T(2,128)(2,1)S(1)}, bf16[2,16512,16,128]{3,2,1,0:T(8,128)(2,1)}) conditional(s32[]{:T(128)} %clamp.61, (pred[2048]{0:T(1024)(128)(4,1)S(1)}, s32[2048]{0:T(1024)S(1)}, pred[2048]{0:T(1024)(128)(4,1)S(1)}, pred[2048]{0:T(1024)(128)(4,1)S(1)}, s32[2048]{0:T(1024)S(1)}, ...), branch_computations={%region_3.4_spmd, %region_4.5_spmd, %region_5.6_spmd, %region_6.7_... | conditional | flops 24576 | bytes 170320 | solution.py:231
  6.2 0.1 copy.69
  6.3 0.1 broadcast_bitcast_fusion.104
  6.4 0.1 broadcast_bitcast_fusion.106
  6.5 0.6 clamp_add_fusion.26.tab_ref
  7.1 698.9 %exchange_61.2 = (bf16[2,16512,8,2,128]{4,3,2,1,0:T(2,128)(2,1)}, bf16[2,8192]{1,0:T(2,128)(2,1)S(1)}) custom-call(s32[2048]{0:T(1024)} %clamp_add_fusion.26.tab_ref, bf16[2,4608]{1,0:T(2,128)(2,1)} %get-tuple-element.3700.x_ref, bf16[4608]{0:T(1024)(128)(2,1)} %get-tuple-element.3701.g_ref, bf16[81920,2,128]{2,1,0:T(2,128)(2,1)} %bitcast.701, ...), custom_call_target="tpu_custom_call" | custom-call | tf_op jit(solution)/shard_map/cond/branch_26_fun/exchange_61/pallas_call | solution.py:210
  706.2 0.0 copy-start
  706.3 0.0 copy-done.1
  706.3 0.1 dynamic-slice_convert_fusion
  706.4 0.1 multiply_cosine_fusion
  706.5 0.1 fusion.6
  706.6 0.7 pad_maximum_fusion.1.kn_ref
  707.3 0.1 fusion.17
  707.4 0.7 pad_maximum_fusion
  708.1 0.6 copy.202
  708.7 36.3 %attend.1 = (bf16[2,32,128]{2,1,0:T(8,128)(2,1)}, bf16[2,4096,16,128]{3,2,1,0:T(8,128)(2,1)}, bf16[2,4096,16,128]{3,2,1,0:T(8,128)(2,1)}) custom-call(s32[16]{0:T(128)} %len_ref.1, bf16[2,32,128]{2,1,0:T(8,128)(2,1)} %bitcast.732, bf16[2,16,128]{2,1,0:T(8,128)(2,1)} %pad_maximum_fusion.1.kn_ref, bf16[2,16,128]{2,1,0:T(8,128)(2,1)} %bitcast.734, ...), custom_call_target="tpu_custom_call" | custom-call | tf_op jit(solution)/shard_map/attend/pallas_call | solution.py:388
  745.0 0.7 copy.201
  745.8 0.0 copy-done
  745.8 14.9 %fusion = bf16[2,4608]{1,0:T(2,128)(2,1)} fusion(bf16[2,4096]{1,0:T(2,128)(2,1)S(1)} %reshape.682, bf16[4096,4608]{1,0:T(8,128)(2,1)} %param.46, bf16[2,4608]{1,0:T(2,128)(2,1)S(1)} %copy-done), kind=kOutput, calls=%fused_computation.253 | convolution fusion | flops 75525120 | bytes 37801984 | tf_op jit(solution)/shard_map/dot_general | solution.py:435
  (21 shorter events, 0.2 us)
Async XLA Ops:
  5.9 700.4 %copy-start.1 = (s32[16]{0:T(128)S(1)}, s32[16]{0:T(128)}, u32[]{:S(2)}) copy-start(s32[16]{0:T(128)} %len_ref.1) | copy-start | bytes 196
  706.2 39.6 %copy-start = (bf16[2,4608]{1,0:T(2,128)(2,1)S(1)}, bf16[2,4608]{1,0:T(2,128)(2,1)}, u32[]{:S(2)}) copy-start(bf16[2,4608]{1,0:T(2,128)(2,1)} %param.41) | copy-start | bytes 55300
